TPU v7x, 32 devices: a whole 2x2x4 slice. The times are simulated.
32 devices in a mesh: rep: 4 (over z), gy: 2 (over y), gz: 4 (over x, core).
Axes of the slice: x: 2, y: 2, z: 4, core: 2. Of those that a mesh axis runs over, the one named last changes fastest.
Arguments:
- charges: float32 [1024, 256, 128], P(('rep', 'gz'), 'gy'), may hold values from -6 to 6
- green: float32 [256, 256, 128], P('rep', ('gy', 'gz')), may hold values from 0.1 to 3
Outputs:
- potential: float32 [1024, 256, 128], P(('rep', 'gz'), 'gy')
All inputs are finite; a program needn't handle non-finite values.
Results may differ from a plain program's by a relative error of at most 0.00007.
Values sent between devices are 32-bit elements; how exact they have to be, the bound alone decides.
A program may use at most 64 MiB of HBM per device.

v0:
```python
import functools
import math

import jax
import jax.numpy as jnp
import numpy as np
from jax import lax
from jax.experimental import pallas as pl
from jax.experimental.pallas import tpu as pltpu
from jax.sharding import PartitionSpec as P

NG = 256
NZ = 128


two_pi = 2.0 * math.pi
highest = lax.Precision.HIGHEST


def tables(length, rows_index, cols_index):
    phase = rows_index[:, None] * cols_index[None, :] % length
    angle = phase.astype(jnp.float32) * (two_pi / length)
    return (jnp.cos(angle), jnp.sin(angle))


def reflect(values):
    return jnp.roll(jnp.flip(values, (1, 2)), (1, 1), axis=(1, 2))


def slab_plan(charges, green):
    gy_count = lax.axis_size("gy")
    gz_count = lax.axis_size("gz")
    groups = gy_count * gz_count
    half = NZ // 2
    per_device = half // groups
    col_block = charges.shape[1]
    depth = jnp.arange(NZ, dtype=jnp.int32)
    bins = jnp.arange(half, dtype=jnp.int32)
    indices = jnp.arange(NG, dtype=jnp.int32)
    cos_depth, sin_depth = tables(NZ, depth, bins)
    alternate = (1 - 2 * (depth % 2)).astype(jnp.float32)
    sin_packed = jnp.where(bins[None, :] == 0, -alternate[:, None], sin_depth)
    spec_re = jnp.einsum("xyz,zk->kxy", charges, cos_depth, precision=highest)
    spec_im = -jnp.einsum("xyz,zk->kxy", charges, sin_packed, precision=highest)
    own = jnp.moveaxis(green[:, :, :half], 2, 0)
    mirror = jnp.concatenate(
        [green[:, :, half : half + 1], jnp.flip(green[:, :, half + 1 :], 2)], axis=2
    )
    mirror = jnp.moveaxis(mirror, 2, 0)
    own, mirror = (
        lax.all_to_all(own, ("gy", "gz"), split_axis=0, concat_axis=2, tiled=True),
        lax.all_to_all(mirror, ("gy", "gz"), split_axis=0, concat_axis=2, tiled=True),
    )
    own, mirror = (
        lax.all_gather(own, "rep", axis=1, tiled=True),
        lax.all_gather(mirror, "rep", axis=1, tiled=True),
    )
    plane_re, plane_im = (
        lax.all_to_all(spec_re, ("gy", "gz"), split_axis=0, concat_axis=1, tiled=True),
        lax.all_to_all(spec_im, ("gy", "gz"), split_axis=0, concat_axis=1, tiled=True),
    )
    plane_re = plane_re.reshape(per_device, gy_count, NG, col_block)
    plane_im = plane_im.reshape(per_device, gy_count, NG, col_block)
    cos_plain, sin_plain = tables(NG, indices, indices)
    wide_cos = cos_plain.reshape(NG, gy_count, col_block)
    wide_sin = sin_plain.reshape(NG, gy_count, col_block)

    def second_in(matrix, values):
        return jnp.einsum("kgc,bgxc->bxk", matrix, values, precision=highest)

    def first_in(matrix, values):
        return jnp.einsum("kx,bxj->bkj", matrix, values, precision=highest)

    inner_re = second_in(wide_cos, plane_re) + second_in(wide_sin, plane_im)
    inner_im = second_in(wide_cos, plane_im) - second_in(wide_sin, plane_re)
    freq_re = first_in(cos_plain, inner_re) + first_in(sin_plain, inner_im)
    freq_im = first_in(cos_plain, inner_im) - first_in(sin_plain, inner_re)
    slot = lax.axis_index("gy") * gz_count + lax.axis_index("gz")
    packed = ((slot == 0) & (jnp.arange(per_device) == 0))[:, None, None]
    plain_gain = 0.5 * (own + reflect(mirror))
    first_gain = jnp.where(packed, 0.5 * (own + reflect(own)), plain_gain)
    second_gain = jnp.where(packed, 0.5 * (mirror + reflect(mirror)), plain_gain)
    mean_gain = 0.5 * (first_gain + second_gain)
    odd_gain = 0.5 * (first_gain - second_gain)
    prod_re = freq_re * mean_gain + reflect(freq_re) * odd_gain
    prod_im = freq_im * mean_gain - reflect(freq_im) * odd_gain
    undo_re = first_in(cos_plain, prod_re) - first_in(sin_plain, prod_im)
    undo_im = first_in(sin_plain, prod_re) + first_in(cos_plain, prod_im)

    def second_out(matrix, values):
        return jnp.einsum("kgc,bxk->bgxc", matrix, values, precision=highest)

    cells_re = second_out(wide_cos, undo_re) - second_out(wide_sin, undo_im)
    cells_im = second_out(wide_sin, undo_re) + second_out(wide_cos, undo_im)
    cells_re = cells_re.reshape(per_device, gy_count * NG, col_block)
    cells_im = cells_im.reshape(per_device, gy_count * NG, col_block)
    home_re, home_im = (
        lax.all_to_all(cells_re, ("gy", "gz"), split_axis=1, concat_axis=0, tiled=True),
        lax.all_to_all(cells_im, ("gy", "gz"), split_axis=1, concat_axis=0, tiled=True),
    )
    weight = jnp.where(bins == 0, 1.0, 2.0).astype(jnp.float32)
    cos_back = (cos_depth * weight[None, :]).T
    sin_back = jnp.where(bins[:, None] == 0, alternate[None, :], -2.0 * sin_depth.T)
    result_field = jnp.einsum("kxy,kz->xyz", home_re, cos_back, precision=highest)
    result_field = result_field + jnp.einsum("kxy,kz->xyz", home_im, sin_back, precision=highest)
    return result_field / (NG * NG * NZ)


f32 = jnp.float32
bf16 = jnp.bfloat16
MESH = pl.DeviceIdType.MESH
PARTS = 2


def split(values):
    high = values.astype(bf16)
    return high, (values - high.astype(f32)).astype(bf16)


def split_table(table):
    rounded = table.astype(jnp.bfloat16)
    high = jnp.asarray(rounded)
    low = jnp.asarray((table - rounded.astype(np.float64)).astype(jnp.bfloat16))
    return high, low


def dot(left, right, dims=((1,), (0,))):
    return lax.dot_general(left, right, (dims, ((), ())), preferred_element_type=f32)


def dot_table(values, table_high, table_low, dims=((1,), (0,))):
    high, low = split(values)
    return dot(high, table_high, dims) + (dot(low, table_high, dims) + dot(high, table_low, dims))


def table_dot(table_high, table_low, values, dims=((1,), (0,))):
    high, low = split(values)
    return dot(table_high, high, dims) + (dot(table_high, low, dims) + dot(table_low, high, dims))


def depth_tables(length, groups, bins_each):
    per_part = bins_each // PARTS
    forward, back = [], []
    z = np.arange(length)
    alternate = 1.0 - 2.0 * (z % 2)
    for start in range(0, groups * bins_each, per_part):
        for imaginary in (False, True):
            for k in range(start, start + per_part):
                angle = 2.0 * np.pi * ((k * z) % length) / length
                if k == 0:
                    forward.append(alternate if imaginary else np.ones(length))
                    back.append(alternate if imaginary else np.ones(length))
                else:
                    forward.append(-np.sin(angle) if imaginary else np.cos(angle))
                    back.append(-2.0 * np.sin(angle) if imaginary else 2.0 * np.cos(angle))
    return np.stack(forward), np.stack(back)


def depth_in_kernel(high_ref, low_ref, cells_ref, out_ref):
    rows, cols, depth = cells_ref.shape
    groups, parts, _, _ = out_ref.shape
    values = cells_ref[...].reshape(rows * cols, depth)
    result = table_dot(high_ref[...], low_ref[...], values, ((1,), (1,)))
    for row in range(rows):
        piece = result[:, row * cols : (row + 1) * cols]
        out_ref[:, :, row * 8 : (row + 1) * 8, :] = piece.reshape(groups, parts, 8, cols)


def depth_out_kernel(high_ref, low_ref, spec_ref, out_ref):
    rows, cols, depth = out_ref.shape
    pieces = [
        spec_ref[:, :, row * 8 : (row + 1) * 8, :].reshape(high_ref.shape[0], cols) for row in range(rows)
    ]
    values = jnp.concatenate(pieces, axis=1)
    result = dot_table(values, high_ref[...], low_ref[...], ((0,), (0,)))
    out_ref[...] = result.reshape(rows, cols, depth)


def planes_kernel(
    gy_count, gz_count, reps,
    spec_ref, gains_ref, mat_h, mat_l, tra_h, tra_l, flip_ref, home_ref,
    planes, green, freq,
    fwd_send, fwd_recv, back_send, back_recv, green_send, green_recv, right_send, left_send, line_recv, own_sem,
):
    groups = gy_count * gz_count
    rep, gy, gz = lax.axis_index("rep"), lax.axis_index("gy"), lax.axis_index("gz")
    slot = gy * gz_count + gz
    rows = spec_ref.shape[2] // 8
    ng = flip_ref.shape[0]
    piece = gains_ref.shape[1]

    def partner(step):
        there_y = lax.rem(gy + step // gz_count, gy_count)
        there_z = lax.rem(gz + step % gz_count, gz_count)
        return there_y * gz_count + there_z, {"rep": rep, "gy": there_y, "gz": there_z}

    def along(step):
        return {"rep": lax.rem(rep + step + reps, reps), "gy": gy, "gz": gz}

    order = sorted(range(1, groups), key=lambda s: (-(s % gz_count), s))

    barrier = pltpu.get_barrier_semaphore()
    for step in order:
        pl.semaphore_signal(barrier, inc=1, device_id=partner(step)[1], device_id_type=MESH)
    for step in (1, -1):
        pl.semaphore_signal(barrier, inc=1, device_id=along(step), device_id_type=MESH)
    pl.semaphore_wait(barrier, groups + 1)

    def green_copy(step, source):
        there, device = partner(step)
        return pltpu.make_async_remote_copy(
            src_ref=gains_ref.at[there], dst_ref=green.at[rep, pl.ds(source * piece, piece), :],
            send_sem=green_send.at[there], recv_sem=green_recv.at[source], device_id=device, device_id_type=MESH)

    def fwd_copy(step, source, part):
        there, device = partner(step)
        return pltpu.make_async_remote_copy(
            src_ref=spec_ref.at[there, part], dst_ref=planes.at[source, part],
            send_sem=fwd_send.at[there, part], recv_sem=fwd_recv.at[source, part], device_id=device, device_id_type=MESH)

    def back_copy(step, source, part):
        there, device = partner(step)
        return pltpu.make_async_remote_copy(
            src_ref=planes.at[there, part], dst_ref=home_ref.at[source, part],
            send_sem=back_send.at[there, part], recv_sem=back_recv.at[source, part], device_id=device, device_id_type=MESH)

    def line_copy(block, sem, step):
        return pltpu.make_async_remote_copy(
            src_ref=green.at[block], dst_ref=green.at[block], send_sem=sem, recv_sem=line_recv.at[block],
            device_id=along(step), device_id_type=MESH)

    for step in order:
        green_copy(step, slot).start()
    own_green = pltpu.make_async_copy(gains_ref.at[slot], green.at[rep, pl.ds(slot * piece, piece), :], own_sem.at[0])
    own_green.start()
    own_planes = [pltpu.make_async_copy(spec_ref.at[slot, h], planes.at[slot, h], own_sem.at[1 + h]) for h in range(PARTS)]
    for copy in own_planes:
        copy.start()
    own_green.wait()
    for step in order:
        green_copy(step, partner(step)[0]).wait_recv()

    @pl.when(rep + 1 < reps)
    def _():
        line_copy(rep, right_send.at[0], 1).start()

    @pl.when(rep >= 1)
    def _():
        line_copy(rep, left_send.at[0], -1).start()

    for part in range(PARTS):
        for step in order:
            fwd_copy(step, slot, part).start()

    def relay(hop):
        @pl.when(rep >= hop)
        def _():
            line_copy(rep - hop, right_send.at[hop], 1).wait_recv()

        @pl.when((rep >= hop) & (rep + 1 < reps))
        def _():
            line_copy(rep - hop, right_send.at[hop], 1).start()

        @pl.when(rep + hop < reps)
        def _():
            line_copy(rep + hop, left_send.at[hop], -1).wait_recv()

        @pl.when((rep + hop < reps) & (rep >= 1))
        def _():
            line_copy(rep + hop, left_send.at[hop], -1).start()

    def load_plane(part, row):
        bands = []
        for y in range(gy_count):
            bands.append(jnp.concatenate(
                [planes[y * gz_count + x, part, pl.ds(row, rows, stride=8), :] for x in range(gz_count)], axis=0))
        return jnp.concatenate(bands, axis=1)

    def forward(part):
        def body(p, carry):
            values = jnp.concatenate([load_plane(part, p), load_plane(part, 4 + p)], axis=1)
            inner = dot_table(values, mat_h[...], mat_l[...])
            inner = jnp.concatenate([inner[:, :ng], inner[:, ng:]], axis=0)
            freq[part * 4 + p] = table_dot(tra_h[...], tra_l[...], inner)
            return carry

        lax.fori_loop(0, 4, body, 0)

    def reflect_plane(values):
        flip = flip_ref[...]
        high, low = split(values)
        turned = dot(flip, high) + dot(flip, low)
        high, low = split(turned)
        return dot(high, flip) + dot(low, flip)

    def backward(part):
        def body(p, carry):
            plane = part * 4 + p
            own, mirror = [], []
            lane = lax.broadcasted_iota(jnp.int32, (ng, 128), 1)
            for r in range(0, reps, 2):
                one = green[r, pl.ds(plane, ng, stride=8), :]
                two = green[r + 1, pl.ds(plane, ng, stride=8), :]
                own.append(jnp.where(lane < 64, one, pltpu.roll(two, 64, 1)))
                mirror.append(jnp.where(lane < 64, pltpu.roll(one, 64, 1), two))
            own = jnp.concatenate(own, axis=1).T
            mirror = jnp.concatenate(mirror, axis=1).T
            packed = (slot == 0) & (plane == 0)

            @pl.when(jnp.logical_not(packed))
            def _():
                gain = 0.5 * (own + reflect_plane(mirror))
                freq[plane] = freq[plane] * jnp.concatenate([gain, gain], axis=0)

            @pl.when(packed)
            def _():
                first = 0.5 * (own + reflect_plane(own))
                second = 0.5 * (mirror + reflect_plane(mirror))
                mean, odd = 0.5 * (first + second), 0.5 * (first - second)
                real, imag = freq[plane, :ng, :], freq[plane, ng:, :]
                freq[plane, :ng, :] = real * mean + reflect_plane(real) * odd
                freq[plane, ng:, :] = imag * mean - reflect_plane(imag) * odd

            undo = table_dot(mat_h[...], mat_l[...], freq[plane])
            undo = jnp.concatenate([undo[:ng], undo[ng:]], axis=1)
            cells = dot_table(undo, tra_h[...], tra_l[...])
            cols = ng // gy_count
            for c in range(2):
                for y in range(gy_count):
                    for x in range(gz_count):
                        planes[y * gz_count + x, part, pl.ds(c * 4 + p, rows, stride=8), :] = cells[
                            x * rows : (x + 1) * rows, c * ng + y * cols : c * ng + (y + 1) * cols]
            return carry

        lax.fori_loop(0, 4, body, 0)

    for part in range(PARTS):
        own_planes[part].wait()
        for step in order:
            fwd_copy(step, partner(step)[0], part).wait_recv()
        forward(part)
        relay(part + 1)
    for hop in range(PARTS + 1, reps):
        relay(hop)

    own_home = [pltpu.make_async_copy(planes.at[slot, h], home_ref.at[slot, h], own_sem.at[1 + h]) for h in range(PARTS)]
    for part in range(PARTS):
        backward(part)
        for step in order:
            back_copy(step, slot, part).start()
        own_home[part].start()
    for step in order:
        green_copy(step, slot).wait_send()
    for part in range(PARTS):
        for step in order:
            fwd_copy(step, slot, part).wait_send()
    for hop in range(reps):
        @pl.when((rep >= hop) & (rep + 1 < reps))
        def _():
            line_copy(rep - hop, right_send.at[hop], 1).wait_send()

        @pl.when((rep + hop < reps) & (rep >= 1))
        def _():
            line_copy(rep + hop, left_send.at[hop], -1).wait_send()
    for part in range(PARTS):
        own_home[part].wait()
        for step in order:
            back_copy(step, slot, part).wait_send()
            back_copy(step, partner(step)[0], part).wait_recv()


def fused_plan(charges, green):
    gy_count, gz_count, reps = lax.axis_size("gy"), lax.axis_size("gz"), lax.axis_size("rep")
    groups = gy_count * gz_count
    rows, cols, depth = charges.shape
    ng = rows * gz_count
    half = depth // 2
    each = half // groups
    step = 8
    forward_table, back_table = depth_tables(depth, groups, each)
    fwd_h, fwd_l = split_table(forward_table)
    back_h, back_l = split_table(back_table / (ng * ng * depth))
    vmem = pl.BlockSpec(memory_space=pltpu.VMEM)
    table_spec = pl.BlockSpec((depth, depth), lambda i: (0, 0))
    cells_spec = pl.BlockSpec((step, cols, depth), lambda i: (i, 0, 0))
    spec_spec = pl.BlockSpec((groups, PARTS, step * 8, cols), lambda i: (0, 0, i, 0))
    spec_shape = jax.ShapeDtypeStruct((groups, PARTS, rows * 8, cols), f32)
    limit = pltpu.CompilerParams(vmem_limit_bytes=40 * 2**20)
    spec = pl.pallas_call(
        depth_in_kernel, grid=(rows // step,), out_shape=spec_shape, name="depth_in",
        in_specs=[table_spec, table_spec, cells_spec], out_specs=spec_spec, compiler_params=limit,
    )(fwd_h, fwd_l, charges)

    k1, k2, _ = green.shape
    own_index = np.arange(half)
    opposite = np.where(own_index == 0, half, depth - own_index)
    pick = np.zeros((2, half, depth), np.float32)
    pick[0, own_index, own_index] = 1.0
    pick[1, own_index, opposite] = 1.0
    gains = jnp.einsum("mqz,xyz->yqmx", jnp.asarray(pick), green, precision=lax.Precision.HIGHEST)
    gains = gains.reshape(k2, groups, each, 2 * k1).transpose(1, 0, 2, 3).reshape(groups, k2 * each, 2 * k1)

    index = np.arange(ng)
    angle = 2.0 * np.pi * ((index[:, None] * index[None, :]) % ng) / ng
    cos, sin = np.cos(angle), np.sin(angle)
    matrix = np.block([[cos, -sin], [sin, cos]])
    mat_h, mat_l = split_table(matrix)
    tra_h, tra_l = split_table(np.ascontiguousarray(matrix.T))
    flip = jnp.asarray((index[:, None] + index[None, :]) % ng == 0, bf16)

    dma = pltpu.SemaphoreType.DMA
    home = pl.pallas_call(
        functools.partial(planes_kernel, gy_count, gz_count, reps),
        out_shape=spec_shape, name="planes",
        in_specs=[vmem] * 7, out_specs=pl.BlockSpec(memory_space=pl.ANY),
        scratch_shapes=[
            pltpu.VMEM(spec_shape.shape, f32),
            pltpu.VMEM((reps, ng * each, 2 * k1), f32),
            pltpu.VMEM((each, 2 * ng, ng), f32),
            dma((groups, PARTS)), dma((groups, PARTS)), dma((groups, PARTS)), dma((groups, PARTS)),
            dma((groups,)), dma((groups,)), dma((reps,)), dma((reps,)), dma((reps,)), dma((1 + PARTS,)),
        ],
        compiler_params=pltpu.CompilerParams(
            collective_id=0, has_side_effects=True, vmem_limit_bytes=58 * 2**20),
    )(spec, gains, mat_h, mat_l, tra_h, tra_l, flip)

    return pl.pallas_call(
        depth_out_kernel, grid=(rows // step,), out_shape=jax.ShapeDtypeStruct(charges.shape, f32), name="depth_out",
        in_specs=[table_spec, table_spec, spec_spec], out_specs=cells_spec, compiler_params=limit,
    )(back_h, back_l, home)


def on_device(charges, green):
    groups = lax.axis_size("gy") * lax.axis_size("gz")
    rows, cols, depth = charges.shape
    aligned = (
        cols % 128 == 0 and depth % 128 == 0 and depth == 16 * groups and rows % 8 == 0
        and green.shape[0] == 64 and lax.axis_size("rep") % 2 == 0 and lax.axis_size("rep") > 2
        and rows * lax.axis_size("gz") == cols * lax.axis_size("gy")
    )
    return fused_plan(charges, green) if aligned else slab_plan(charges, green)


def solution(mesh):
    placed = (P(("rep", "gz"), "gy", None), P("rep", ("gy", "gz"), None))
    return jax.shard_map(
        on_device,
        mesh=mesh,
        in_specs=placed,
        out_specs=P(("rep", "gz"), "gy", None),
        check_vma=False,
    )
```

profile of v0, /device:TPU:0, one launch (start us, length us, event | category | flops | bytes accessed | tf_op | source)
XLA Modules:
  0.0 163.1 jit_solution(15325168626734091070)
XLA Ops:
  0.0 4.6 %convolution_bitcast_fusion = f32[32,64,2,64]{3,1,0,2:T(8,128)S(1)} fusion(f32[2,64,128,1]{2,1,3,0:T(8,128)} %constant.30, f32[64,32,128]{2,1,0:T(8,128)} %param.13), kind=kOutput, calls=%fused_computation | convolution fusion | flops 402653184 | bytes 2162688 | tf_op jit(solution)/shard_map/mqz,xyz->yqmx/dot_general | solution.py:400
  4.6 0.0 copy-start.5
  4.6 0.0 copy-start.6
  4.7 1.7 %copy.15 = f32[32,64,2,64]{3,2,1,0:T(2,128)S(1)} copy(f32[32,64,2,64]{3,1,0,2:T(8,128)S(1)} %convolution_bitcast_fusion) | data formatting | bytes 2097152 | tf_op jit(solution)/shard_map/mqz,xyz->yqmx/transpose | solution.py:400
  6.3 1.1 reshape.6
  7.5 1.0 copy_bitcast_fusion.gains_ref
  8.5 0.0 copy-done.5
  8.5 0.0 copy-done.6
  8.5 0.0 copy-start.2
  8.5 2.2 %copy-done.2 = f32[64,128,128]{2,1,0:T(8,128)S(1)} copy-done((f32[64,128,128]{2,1,0:T(8,128)S(1)}, f32[64,128,128]{2,1,0:T(8,128)}, u32[]{:S(2)}) %copy-start.2) | copy-done | bytes 4194328
  10.7 3.2 %depth_in.1.spec_ref = f32[8,2,512,128]{3,2,1,0:T(8,128)S(1)} custom-call(bf16[128,128]{1,0:T(8,128)(2,1)S(1)} %copy-done.6, bf16[128,128]{1,0:T(8,128)(2,1)S(1)} %copy-done.5, f32[64,128,128]{2,1,0:T(8,128)S(1)} %copy-done.2), custom_call_target="tpu_custom_call" | custom-call | tf_op jit(solution)/shard_map/depth_in/pallas_call | solution.py:389
  14.0 0.0 copy-start.1
  14.0 2.0 %copy-done.1 = f32[8,2,512,128]{3,2,1,0:T(8,128)} copy-done((f32[8,2,512,128]{3,2,1,0:T(8,128)}, f32[8,2,512,128]{3,2,1,0:T(8,128)S(1)}, u32[]{:S(2)}) %copy-start.1) | copy-done | bytes 4194328
  16.0 0.0 copy-start.3
  16.0 0.0 copy-start.4
  16.0 139.5 %planes.1.spec_ref = f32[8,2,512,128]{3,2,1,0:T(8,128)} custom-call(f32[8,2,512,128]{3,2,1,0:T(8,128)} %copy-done.1, f32[8,256,128]{2,1,0:T(8,128)} %copy_bitcast_fusion.gains_ref, bf16[512,512]{1,0:T(8,128)(2,1)} %constant.25.clone.mat_h, bf16[512,512]{1,0:T(8,128)(2,1)} %constant.26.clone.mat_l, bf16[512,512]{1,0:T(8,128)(2,1)} %constant.27.clone.tra_h, ...), custom_call_target="tpu_custom_call" | custom-call | tf_op jit(solution)/shard_map/planes/pallas_call | solution.py:412
  155.5 0.0 copy-done.3
  155.5 0.0 copy-done.4
  155.5 0.0 copy-start
  155.5 2.2 %copy-done = f32[8,2,512,128]{3,2,1,0:T(8,128)S(1)} copy-done((f32[8,2,512,128]{3,2,1,0:T(8,128)S(1)}, f32[8,2,512,128]{3,2,1,0:T(8,128)}, u32[]{:S(2)}) %copy-start) | copy-done | bytes 4194328
  157.7 5.4 %depth_out.1 = f32[64,128,128]{2,1,0:T(8,128)} custom-call(bf16[128,128]{1,0:T(8,128)(2,1)S(1)} %copy-done.4, bf16[128,128]{1,0:T(8,128)(2,1)S(1)} %copy-done.3, f32[8,2,512,128]{3,2,1,0:T(8,128)S(1)} %copy-done), custom_call_target="tpu_custom_call" | custom-call | tf_op jit(solution)/shard_map/depth_out/pallas_call | solution.py:427
Async XLA Ops:
  4.6 3.9 %copy-start.5 = (bf16[128,128]{1,0:T(8,128)(2,1)S(1)}, bf16[128,128]{1,0:T(8,128)(2,1)}, u32[]{:S(2)}) copy-start(bf16[128,128]{1,0:T(8,128)(2,1)} %constant.21.clone.low_ref) | copy-start | bytes 98308
  4.6 3.9 %copy-start.6 = (bf16[128,128]{1,0:T(8,128)(2,1)S(1)}, bf16[128,128]{1,0:T(8,128)(2,1)}, u32[]{:S(2)}) copy-start(bf16[128,128]{1,0:T(8,128)(2,1)} %constant.20.clone.high_ref) | copy-start | bytes 98308
  8.5 2.2 %copy-start.2 = (f32[64,128,128]{2,1,0:T(8,128)S(1)}, f32[64,128,128]{2,1,0:T(8,128)}, u32[]{:S(2)}) copy-start(f32[64,128,128]{2,1,0:T(8,128)} %cells_ref.1) | copy-start | bytes 12582916
  14.0 2.0 %copy-start.1 = (f32[8,2,512,128]{3,2,1,0:T(8,128)}, f32[8,2,512,128]{3,2,1,0:T(8,128)S(1)}, u32[]{:S(2)}) copy-start(f32[8,2,512,128]{3,2,1,0:T(8,128)S(1)} %depth_in.1.spec_ref) | copy-start | bytes 12582916
  16.0 139.5 %copy-start.3 = (bf16[128,128]{1,0:T(8,128)(2,1)S(1)}, bf16[128,128]{1,0:T(8,128)(2,1)}, u32[]{:S(2)}) copy-start(bf16[128,128]{1,0:T(8,128)(2,1)} %constant.23.clone.low_ref) | copy-start | bytes 98308
  16.0 139.5 %copy-start.4 = (bf16[128,128]{1,0:T(8,128)(2,1)S(1)}, bf16[128,128]{1,0:T(8,128)(2,1)}, u32[]{:S(2)}) copy-start(bf16[128,128]{1,0:T(8,128)(2,1)} %constant.22.clone.high_ref) | copy-start | bytes 98308
  155.5 2.2 %copy-start = (f32[8,2,512,128]{3,2,1,0:T(8,128)S(1)}, f32[8,2,512,128]{3,2,1,0:T(8,128)}, u32[]{:S(2)}) copy-start(f32[8,2,512,128]{3,2,1,0:T(8,128)} %planes.1.spec_ref) | copy-start | bytes 12582916
where the time goes:
time: 163 us
  Pallas kernels  148 us (91%)
  local copies, waits for them, and re-layouts  10.2 us (6%)
  matrix products  4.63 us (3%)
    pallas_call x1, Pallas kernels, fused_plan(): pl.pallas_call(functools.partial(planes_kernel, gy_count, gz_count, reps)...  139 us
    unnamed x14, local copies, waits for them, and re-layouts  6.4 us
    pallas_call x1, Pallas kernels, fused_plan(): pl.pallas_call(depth_out_kernel, grid=(rows // step,), out_shape=jax.Shap...  5.4 us
    dot_general x1, matrix products, fused_plan(): jnp.einsum('mqz,xyz->yqmx', jnp.asarray(pick), green, precision=lax.Preci...  4.63 us

commit v1 on v0

--- a/solution.py
+++ b/solution.py
@@ -176,18 +176,39 @@
     out_ref[...] = result.reshape(rows, cols, depth)
 
 
+def pick_kernel(pick_ref, green_ref, out_ref):
+    groups, parts, _, _ = out_ref.shape
+    count = green_ref.shape[0] // 64
+    rest = jnp.concatenate([green_ref[pl.ds(k2, 64, stride=count), :] for k2 in range(count)], axis=0)
+    result = None
+    for _ in range(3):
+        high = rest.astype(bf16)
+        rest = rest - high.astype(f32)
+        term = dot(pick_ref[...], high, ((1,), (1,)))
+        result = term if result is None else result + term
+    size = groups * parts * 8
+    first_lanes = lax.broadcasted_iota(jnp.int32, (size, 128), 1) < 64
+    first_rows = lax.rem(lax.broadcasted_iota(jnp.int32, (size, 128), 0), 8) < 4
+    for pair in range(count // 2):
+        own = result[:size, pair * 128 : (pair + 1) * 128]
+        mirror = result[size:, pair * 128 : (pair + 1) * 128]
+        even = jnp.where(first_lanes, own, pltpu.roll(mirror, 64, 1))
+        odd = jnp.where(first_lanes, pltpu.roll(own, 64, 1), mirror)
+        out_ref[:, :, pair * 8 : (pair + 1) * 8, :] = jnp.where(first_rows, even, odd).reshape(groups, parts, 8, 128)
+
+
 def planes_kernel(
     gy_count, gz_count, reps,
-    spec_ref, gains_ref, mat_h, mat_l, tra_h, tra_l, flip_ref, home_ref,
-    planes, green, freq,
-    fwd_send, fwd_recv, back_send, back_recv, green_send, green_recv, right_send, left_send, line_recv, own_sem,
+    spec_ref, gains_ref, waves_ref, flips_ref, home_ref,
+    planes, green, freq, tables, flips,
+    fwd_send, fwd_recv, back_send, back_recv, green_send, green_recv, right_send, left_send, line_recv, own_sem, table_sem,
 ):
     groups = gy_count * gz_count
     rep, gy, gz = lax.axis_index("rep"), lax.axis_index("gy"), lax.axis_index("gz")
     slot = gy * gz_count + gz
     rows = spec_ref.shape[2] // 8
-    ng = flip_ref.shape[0]
-    piece = gains_ref.shape[1]
+    ng = flips_ref.shape[1]
+    piece = gains_ref.shape[2]
 
     def partner(step):
         there_y = lax.rem(gy + step // gz_count, gy_count)
@@ -196,6 +217,18 @@
 
     def along(step):
         return {"rep": lax.rem(rep + step + reps, reps), "gy": gy, "gz": gz}
+
+    loads = []
+    for table, (kind, swap) in enumerate(((1, False), (0, True), (0, False), (2, True))):
+        minus, plus = (1, 2) if swap else (2, 1)
+        for quadrant, wave in enumerate((0, minus, plus, 0)):
+            loads.append(pltpu.make_async_copy(
+                waves_ref.at[3 * kind + wave],
+                tables.at[table, :, pl.ds(quadrant // 2 * ng, ng), pl.ds(quadrant % 2 * ng, ng)],
+                table_sem.at[4 * table + quadrant]))
+    loads.append(pltpu.make_async_copy(flips_ref, flips, table_sem.at[16]))
+    for load in loads:
+        load.start()
 
     order = sorted(range(1, groups), key=lambda s: (-(s % gz_count), s))
 
@@ -206,11 +239,11 @@
         pl.semaphore_signal(barrier, inc=1, device_id=along(step), device_id_type=MESH)
     pl.semaphore_wait(barrier, groups + 1)
 
-    def green_copy(step, source):
+    def green_copy(step, source, part):
         there, device = partner(step)
         return pltpu.make_async_remote_copy(
-            src_ref=gains_ref.at[there], dst_ref=green.at[rep, pl.ds(source * piece, piece), :],
-            send_sem=green_send.at[there], recv_sem=green_recv.at[source], device_id=device, device_id_type=MESH)
+            src_ref=gains_ref.at[there, part], dst_ref=green.at[rep, part, pl.ds(source * piece, piece), :],
+            send_sem=green_send.at[there, part], recv_sem=green_recv.at[source, part], device_id=device, device_id_type=MESH)
 
     def fwd_copy(step, source, part):
         there, device = partner(step)
@@ -224,50 +257,48 @@
             src_ref=planes.at[there, part], dst_ref=home_ref.at[source, part],
             send_sem=back_send.at[there, part], recv_sem=back_recv.at[source, part], device_id=device, device_id_type=MESH)
 
-    def line_copy(block, sem, step):
+    def line_copy(block, part, sem, step):
         return pltpu.make_async_remote_copy(
-            src_ref=green.at[block], dst_ref=green.at[block], send_sem=sem, recv_sem=line_recv.at[block],
-            device_id=along(step), device_id_type=MESH)
-
-    for step in order:
-        green_copy(step, slot).start()
-    own_green = pltpu.make_async_copy(gains_ref.at[slot], green.at[rep, pl.ds(slot * piece, piece), :], own_sem.at[0])
-    own_green.start()
-    own_planes = [pltpu.make_async_copy(spec_ref.at[slot, h], planes.at[slot, h], own_sem.at[1 + h]) for h in range(PARTS)]
-    for copy in own_planes:
+            src_ref=green.at[block, part], dst_ref=green.at[block, part], send_sem=sem.at[part],
+            recv_sem=line_recv.at[block, part], device_id=along(step), device_id_type=MESH)
+
+    own_green = [
+        pltpu.make_async_copy(
+            gains_ref.at[slot, h], green.at[rep, h, pl.ds(slot * piece, piece), :], own_sem.at[PARTS + h])
+        for h in range(PARTS)
+    ]
+    own_planes = [pltpu.make_async_copy(spec_ref.at[slot, h], planes.at[slot, h], own_sem.at[h]) for h in range(PARTS)]
+    for part in range(PARTS):
+        for step in order:
+            green_copy(step, slot, part).start()
+    for copy in own_green + own_planes:
         copy.start()
-    own_green.wait()
-    for step in order:
-        green_copy(step, partner(step)[0]).wait_recv()
-
-    @pl.when(rep + 1 < reps)
-    def _():
-        line_copy(rep, right_send.at[0], 1).start()
-
-    @pl.when(rep >= 1)
-    def _():
-        line_copy(rep, left_send.at[0], -1).start()
-
-    for part in range(PARTS):
-        for step in order:
-            fwd_copy(step, slot, part).start()
-
-    def relay(hop):
+
+    def line_start(part):
+        @pl.when(rep + 1 < reps)
+        def _():
+            line_copy(rep, part, right_send.at[0], 1).start()
+
+        @pl.when(rep >= 1)
+        def _():
+            line_copy(rep, part, left_send.at[0], -1).start()
+
+    def relay(hop, part):
         @pl.when(rep >= hop)
         def _():
-            line_copy(rep - hop, right_send.at[hop], 1).wait_recv()
+            line_copy(rep - hop, part, right_send.at[hop], 1).wait_recv()
 
         @pl.when((rep >= hop) & (rep + 1 < reps))
         def _():
-            line_copy(rep - hop, right_send.at[hop], 1).start()
+            line_copy(rep - hop, part, right_send.at[hop], 1).start()
 
         @pl.when(rep + hop < reps)
         def _():
-            line_copy(rep + hop, left_send.at[hop], -1).wait_recv()
+            line_copy(rep + hop, part, left_send.at[hop], -1).wait_recv()
 
         @pl.when((rep + hop < reps) & (rep >= 1))
         def _():
-            line_copy(rep + hop, left_send.at[hop], -1).start()
+            line_copy(rep + hop, part, left_send.at[hop], -1).start()
 
     def load_plane(part, row):
         bands = []
@@ -279,19 +310,18 @@
     def forward(part):
         def body(p, carry):
             values = jnp.concatenate([load_plane(part, p), load_plane(part, 4 + p)], axis=1)
-            inner = dot_table(values, mat_h[...], mat_l[...])
+            inner = dot_table(values, tables[0, 0], tables[0, 1])
             inner = jnp.concatenate([inner[:, :ng], inner[:, ng:]], axis=0)
-            freq[part * 4 + p] = table_dot(tra_h[...], tra_l[...], inner)
+            freq[part * 4 + p] = table_dot(tables[1, 0], tables[1, 1], inner)
             return carry
 
         lax.fori_loop(0, 4, body, 0)
 
     def reflect_plane(values):
-        flip = flip_ref[...]
         high, low = split(values)
-        turned = dot(flip, high) + dot(flip, low)
+        turned = dot(flips[0], high) + dot(flips[0], low)
         high, low = split(turned)
-        return dot(high, flip) + dot(low, flip)
+        return dot(high, flips[1]) + dot(low, flips[1])
 
     def backward(part):
         def body(p, carry):
@@ -299,8 +329,10 @@
             own, mirror = [], []
             lane = lax.broadcasted_iota(jnp.int32, (ng, 128), 1)
             for r in range(0, reps, 2):
-                one = green[r, pl.ds(plane, ng, stride=8), :]
-                two = green[r + 1, pl.ds(plane, ng, stride=8), :]
+                one, two = (
+                    jnp.concatenate([green[q, part, pl.ds(4 * odd + p, ng // 2, stride=8), :] for odd in range(2)], axis=0)
+                    for q in (r, r + 1)
+                )
                 own.append(jnp.where(lane < 64, one, pltpu.roll(two, 64, 1)))
                 mirror.append(jnp.where(lane < 64, pltpu.roll(one, 64, 1), two))
             own = jnp.concatenate(own, axis=1).T
@@ -321,9 +353,9 @@
                 freq[plane, :ng, :] = real * mean + reflect_plane(real) * odd
                 freq[plane, ng:, :] = imag * mean - reflect_plane(imag) * odd
 
-            undo = table_dot(mat_h[...], mat_l[...], freq[plane])
+            undo = table_dot(tables[2, 0], tables[2, 1], freq[plane])
             undo = jnp.concatenate([undo[:ng], undo[ng:]], axis=1)
-            cells = dot_table(undo, tra_h[...], tra_l[...])
+            cells = dot_table(undo, tables[3, 0], tables[3, 1])
             cols = ng // gy_count
             for c in range(2):
                 for y in range(gy_count):
@@ -334,34 +366,54 @@
 
         lax.fori_loop(0, 4, body, 0)
 
-    for part in range(PARTS):
+    own_home = [pltpu.make_async_copy(planes.at[slot, h], home_ref.at[slot, h], own_sem.at[h]) for h in range(PARTS)]
+
+    def arrive(part):
         own_planes[part].wait()
         for step in order:
             fwd_copy(step, partner(step)[0], part).wait_recv()
         forward(part)
-        relay(part + 1)
-    for hop in range(PARTS + 1, reps):
-        relay(hop)
-
-    own_home = [pltpu.make_async_copy(planes.at[slot, h], home_ref.at[slot, h], own_sem.at[1 + h]) for h in range(PARTS)]
-    for part in range(PARTS):
+
+    def depart(part):
         backward(part)
         for step in order:
             back_copy(step, slot, part).start()
         own_home[part].start()
-    for step in order:
-        green_copy(step, slot).wait_send()
+
     for part in range(PARTS):
-        for step in order:
+        own_green[part].wait()
+        for step in order:
+            green_copy(step, partner(step)[0], part).wait_recv()
+        if part == 0:
+            line_start(0)
+    for part in range(PARTS):
+        for step in order:
+            fwd_copy(step, slot, part).start()
+    for hop in range(1, reps):
+        relay(hop, 0)
+    line_start(1)
+    for load in loads:
+        load.wait()
+    arrive(0)
+    depart(0)
+    relay(1, 1)
+    arrive(1)
+    for hop in range(2, reps):
+        relay(hop, 1)
+    depart(1)
+
+    for part in range(PARTS):
+        for step in order:
+            green_copy(step, slot, part).wait_send()
             fwd_copy(step, slot, part).wait_send()
-    for hop in range(reps):
-        @pl.when((rep >= hop) & (rep + 1 < reps))
-        def _():
-            line_copy(rep - hop, right_send.at[hop], 1).wait_send()
-
-        @pl.when((rep + hop < reps) & (rep >= 1))
-        def _():
-            line_copy(rep + hop, left_send.at[hop], -1).wait_send()
+        for hop in range(reps):
+            @pl.when((rep >= hop) & (rep + 1 < reps))
+            def _():
+                line_copy(rep - hop, part, right_send.at[hop], 1).wait_send()
+
+            @pl.when((rep + hop < reps) & (rep >= 1))
+            def _():
+                line_copy(rep + hop, part, left_send.at[hop], -1).wait_send()
     for part in range(PARTS):
         own_home[part].wait()
         for step in order:
@@ -394,35 +446,44 @@
     k1, k2, _ = green.shape
     own_index = np.arange(half)
     opposite = np.where(own_index == 0, half, depth - own_index)
-    pick = np.zeros((2, half, depth), np.float32)
-    pick[0, own_index, own_index] = 1.0
-    pick[1, own_index, opposite] = 1.0
-    gains = jnp.einsum("mqz,xyz->yqmx", jnp.asarray(pick), green, precision=lax.Precision.HIGHEST)
-    gains = gains.reshape(k2, groups, each, 2 * k1).transpose(1, 0, 2, 3).reshape(groups, k2 * each, 2 * k1)
+    quads = np.repeat(np.arange(half // 4), 8) * 4 + np.tile(np.arange(4), half // 2)
+    pick = np.zeros((2 * depth, depth), np.float32)
+    pick[np.arange(depth), own_index[quads]] = 1.0
+    pick[depth + np.arange(depth), opposite[quads]] = 1.0
+    gains = pl.pallas_call(
+        pick_kernel, out_shape=jax.ShapeDtypeStruct((groups, PARTS, k2 * 4, 2 * k1), f32), name="pick",
+        in_specs=[vmem, vmem], out_specs=vmem, compiler_params=limit,
+    )(jnp.asarray(pick, bf16), green.reshape(k1 * k2, depth))
 
     index = np.arange(ng)
+    halves = np.concatenate([index[0::2], index[1::2]])
     angle = 2.0 * np.pi * ((index[:, None] * index[None, :]) % ng) / ng
     cos, sin = np.cos(angle), np.sin(angle)
-    matrix = np.block([[cos, -sin], [sin, cos]])
-    mat_h, mat_l = split_table(matrix)
-    tra_h, tra_l = split_table(np.ascontiguousarray(matrix.T))
-    flip = jnp.asarray((index[:, None] + index[None, :]) % ng == 0, bf16)
+    waves = np.stack([cos, sin, -sin])
+    waves = np.concatenate([waves, waves[:, :, halves], waves[:, halves, :]])
+    rounded = waves.astype(jnp.bfloat16)
+    waves = jnp.asarray(np.stack([rounded, (waves - rounded.astype(np.float64)).astype(jnp.bfloat16)], axis=1))
+    flips = np.stack([(rows_of[:, None] + rows_of[None, :]) % ng == 0 for rows_of in (index, halves)])
+    flips = jnp.asarray(flips, bf16)
 
     dma = pltpu.SemaphoreType.DMA
+    both = (groups, PARTS)
     home = pl.pallas_call(
         functools.partial(planes_kernel, gy_count, gz_count, reps),
         out_shape=spec_shape, name="planes",
-        in_specs=[vmem] * 7, out_specs=pl.BlockSpec(memory_space=pl.ANY),
+        in_specs=[pl.BlockSpec(memory_space=pl.ANY)] * 4, out_specs=pl.BlockSpec(memory_space=pl.ANY),
         scratch_shapes=[
             pltpu.VMEM(spec_shape.shape, f32),
-            pltpu.VMEM((reps, ng * each, 2 * k1), f32),
+            pltpu.VMEM((reps, PARTS, ng * each // PARTS, 2 * k1), f32),
             pltpu.VMEM((each, 2 * ng, ng), f32),
-            dma((groups, PARTS)), dma((groups, PARTS)), dma((groups, PARTS)), dma((groups, PARTS)),
-            dma((groups,)), dma((groups,)), dma((reps,)), dma((reps,)), dma((reps,)), dma((1 + PARTS,)),
+            pltpu.VMEM((4, 2, 2 * ng, 2 * ng), bf16),
+            pltpu.VMEM((2, ng, ng), bf16),
+            dma(both), dma(both), dma(both), dma(both), dma(both), dma(both),
+            dma((reps, PARTS)), dma((reps, PARTS)), dma((reps, PARTS)), dma((2 * PARTS,)), dma((17,)),
         ],
         compiler_params=pltpu.CompilerParams(
-            collective_id=0, has_side_effects=True, vmem_limit_bytes=58 * 2**20),
-    )(spec, gains, mat_h, mat_l, tra_h, tra_l, flip)
+            collective_id=0, has_side_effects=True, vmem_limit_bytes=63 * 2**20),
+    )(spec, gains, waves, flips)
 
     return pl.pallas_call(
         depth_out_kernel, grid=(rows // step,), out_shape=jax.ShapeDtypeStruct(charges.shape, f32), name="depth_out",

time: 163 us -> 133 us (0.82)
  Pallas kernels: 148 us -> 122 us
  matrix products: 4.63 us -> 0 us
    pallas_call x1, Pallas kernels: 139 us -> 111 us  [fused_plan(): pl.pallas_call(functools.partial(planes_kernel, gy_count, gz_count, reps)...]
    dot_general x1 -> x0, matrix products: 4.63 us -> none  [fused_plan(): jnp.einsum('mqz,xyz->yqmx', jnp.asarray(pick), green, precision=lax.Preci...]
    unnamed x14 -> x20, local copies, waits for them, and re-layouts: 6.4 us -> 10.9 us
    reshape x2 -> x0, local copies, waits for them, and re-layouts: 2.18 us -> none  [fused_plan(): gains.reshape(k2, groups, each, 2 * k1).transpose(1, 0, 2, 3)]
    pallas_call x0 -> x1, Pallas kernels: none -> 1.78 us  [fused_plan(): pl.pallas_call(pick_kernel, out_shape=jax.ShapeDtypeStruct((groups, PARTS...]
    transpose x1 -> x0, local copies, waits for them, and re-layouts: 1.67 us -> none  [fused_plan(): jnp.einsum('mqz,xyz->yqmx', jnp.asarray(pick), green, precision=lax.Preci...]
where the time goes in v1:
time: 133 us
  Pallas kernels  122 us (92%)
  local copies, waits for them, and re-layouts  10.9 us (8%)
    pallas_call x1, Pallas kernels, fused_plan(): pl.pallas_call(functools.partial(planes_kernel, gy_count, gz_count, reps)...  111 us
    unnamed x20, local copies, waits for them, and re-layouts  10.9 us
    pallas_call x1, Pallas kernels, fused_plan(): pl.pallas_call(depth_out_kernel, grid=(rows // step,), out_shape=jax.Shap...  5.4 us
    pallas_call x1, Pallas kernels, fused_plan(): pl.pallas_call(depth_in_kernel, grid=(rows // step,), out_shape=spec_shap...  3.24 us

profile of v1, /device:TPU:0, one launch (start us, length us, event | category | flops | bytes accessed | tf_op | source)
XLA Modules:
  0.0 132.7 jit_solution(13723738551880300783)
XLA Ops:
  0.0 0.0 copy-start.4
  0.0 1.2 copy-done.4
  1.2 0.0 copy-start.5
  1.2 0.8 copy-done.5
  2.1 1.8 %pick.1.gains_ref = f32[8,2,128,128]{3,2,1,0:T(8,128)S(1)} custom-call(bf16[256,128]{1,0:T(8,128)(2,1)S(1)} %copy-done.5, f32[2048,128]{1,0:T(8,128)S(1)} %bitcast.1), custom_call_target="tpu_custom_call" | custom-call | tf_op jit(solution)/shard_map/pick/pallas_call | solution.py:453
  3.9 0.0 copy-start.2
  3.9 1.0 copy-done.2
  4.8 0.0 copy-start.3
  4.8 2.2 %copy-done.3 = f32[64,128,128]{2,1,0:T(8,128)S(1)} copy-done((f32[64,128,128]{2,1,0:T(8,128)S(1)}, f32[64,128,128]{2,1,0:T(8,128)}, u32[]{:S(2)}) %copy-start.3) | copy-done | bytes 4194328
  7.0 0.0 copy-start.8
  7.0 0.8 copy-done.8
  7.8 0.0 copy-start.9
  7.8 0.8 copy-done.9
  8.5 3.2 %depth_in.1.spec_ref = f32[8,2,512,128]{3,2,1,0:T(8,128)S(1)} custom-call(bf16[128,128]{1,0:T(8,128)(2,1)S(1)} %copy-done.9, bf16[128,128]{1,0:T(8,128)(2,1)S(1)} %copy-done.8, f32[64,128,128]{2,1,0:T(8,128)S(1)} %copy-done.3), custom_call_target="tpu_custom_call" | custom-call | tf_op jit(solution)/shard_map/depth_in/pallas_call | solution.py:441
  11.8 0.0 copy-start.1
  11.8 2.0 %copy-done.1 = f32[8,2,512,128]{3,2,1,0:T(8,128)} copy-done((f32[8,2,512,128]{3,2,1,0:T(8,128)}, f32[8,2,512,128]{3,2,1,0:T(8,128)S(1)}, u32[]{:S(2)}) %copy-start.1) | copy-done | bytes 4194328
  13.8 0.0 copy-start.6
  13.8 0.0 copy-start.7
  13.8 111.3 %planes.1.spec_ref = f32[8,2,512,128]{3,2,1,0:T(8,128)} custom-call(f32[8,2,512,128]{3,2,1,0:T(8,128)} %copy-done.1, f32[8,2,128,128]{3,2,1,0:T(8,128)} %copy-done.2, bf16[9,2,256,256]{3,2,1,0:T(8,128)(2,1)} %constant.19.clone.waves_ref, bf16[2,256,256]{2,1,0:T(8,128)(2,1)} %constant.20.clone.flips_ref), custom_call_target="tpu_custom_call" | custom-call | tf_op jit(solution)/shard_map/planes/pallas_call | solution.py:471
  125.1 0.0 copy-done.6
  125.1 0.0 copy-done.7
  125.2 0.0 copy-start
  125.2 2.2 %copy-done = f32[8,2,512,128]{3,2,1,0:T(8,128)S(1)} copy-done((f32[8,2,512,128]{3,2,1,0:T(8,128)S(1)}, f32[8,2,512,128]{3,2,1,0:T(8,128)}, u32[]{:S(2)}) %copy-start) | copy-done | bytes 4194328
  127.3 5.4 %depth_out.1 = f32[64,128,128]{2,1,0:T(8,128)} custom-call(bf16[128,128]{1,0:T(8,128)(2,1)S(1)} %copy-done.7, bf16[128,128]{1,0:T(8,128)(2,1)S(1)} %copy-done.6, f32[8,2,512,128]{3,2,1,0:T(8,128)S(1)} %copy-done), custom_call_target="tpu_custom_call" | custom-call | tf_op jit(solution)/shard_map/depth_out/pallas_call | solution.py:488
Async XLA Ops:
  0.0 1.2 copy-start.4
  1.2 0.8 copy-start.5
  3.9 1.0 copy-start.2
  4.8 2.2 %copy-start.3 = (f32[64,128,128]{2,1,0:T(8,128)S(1)}, f32[64,128,128]{2,1,0:T(8,128)}, u32[]{:S(2)}) copy-start(f32[64,128,128]{2,1,0:T(8,128)} %cells_ref.1) | copy-start | bytes 12582916
  7.0 0.8 copy-start.8
  7.8 0.8 copy-start.9
  11.8 2.0 %copy-start.1 = (f32[8,2,512,128]{3,2,1,0:T(8,128)}, f32[8,2,512,128]{3,2,1,0:T(8,128)S(1)}, u32[]{:S(2)}) copy-start(f32[8,2,512,128]{3,2,1,0:T(8,128)S(1)} %depth_in.1.spec_ref) | copy-start | bytes 12582916
  13.8 111.4 %copy-start.6 = (bf16[128,128]{1,0:T(8,128)(2,1)S(1)}, bf16[128,128]{1,0:T(8,128)(2,1)}, u32[]{:S(2)}) copy-start(bf16[128,128]{1,0:T(8,128)(2,1)} %constant.17.clone.low_ref) | copy-start | bytes 98308
  13.8 111.4 %copy-start.7 = (bf16[128,128]{1,0:T(8,128)(2,1)S(1)}, bf16[128,128]{1,0:T(8,128)(2,1)}, u32[]{:S(2)}) copy-start(bf16[128,128]{1,0:T(8,128)(2,1)} %constant.16.clone.high_ref) | copy-start | bytes 98308
  125.2 2.2 %copy-start = (f32[8,2,512,128]{3,2,1,0:T(8,128)S(1)}, f32[8,2,512,128]{3,2,1,0:T(8,128)}, u32[]{:S(2)}) copy-start(f32[8,2,512,128]{3,2,1,0:T(8,128)} %planes.1.spec_ref) | copy-start | bytes 12582916

commit v2 on v1

--- a/solution.py
+++ b/solution.py
@@ -117,6 +117,11 @@
     return high, (values - high.astype(f32)).astype(bf16)
 
 
+def stacked_table(table, axis):
+    rounded = table.astype(jnp.bfloat16)
+    return jnp.asarray(np.stack([rounded, (table - rounded.astype(np.float64)).astype(jnp.bfloat16)], axis=axis))
+
+
 def split_table(table):
     rounded = table.astype(jnp.bfloat16)
     high = jnp.asarray(rounded)
@@ -156,14 +161,20 @@
     return np.stack(forward), np.stack(back)
 
 
-def depth_in_kernel(high_ref, low_ref, cells_ref, out_ref):
-    rows, cols, depth = cells_ref.shape
-    groups, parts, _, _ = out_ref.shape
-    values = cells_ref[...].reshape(rows * cols, depth)
-    result = table_dot(high_ref[...], low_ref[...], values, ((1,), (1,)))
-    for row in range(rows):
-        piece = result[:, row * cols : (row + 1) * cols]
-        out_ref[:, :, row * 8 : (row + 1) * 8, :] = piece.reshape(groups, parts, 8, cols)
+def depth_in(table, cells, out):
+    groups, parts, _, cols = out.shape
+    rows, depth, step = cells.shape[0], cells.shape[2], 8
+
+    def body(i, carry):
+        values = cells[pl.ds(i * step, step)].reshape(step * cols, depth)
+        result = table_dot(table[0], table[1], values, ((1,), (1,)))
+        for row in range(step):
+            piece = result[:, row * cols : (row + 1) * cols]
+            at = pl.multiple_of(i * (step * 8) + row * 8, 8)
+            out[:, :, pl.ds(at, 8), :] = piece.reshape(groups, parts, 8, cols)
+        return carry
+
+    lax.fori_loop(0, rows // step, body, 0)
 
 
 def depth_out_kernel(high_ref, low_ref, spec_ref, out_ref):
@@ -176,7 +187,7 @@
     out_ref[...] = result.reshape(rows, cols, depth)
 
 
-def pick_kernel(pick_ref, green_ref, out_ref):
+def pick_green(pick_ref, green_ref, out_ref):
     groups, parts, _, _ = out_ref.shape
     count = green_ref.shape[0] // 64
     rest = jnp.concatenate([green_ref[pl.ds(k2, 64, stride=count), :] for k2 in range(count)], axis=0)
@@ -199,9 +210,10 @@
 
 def planes_kernel(
     gy_count, gz_count, reps,
-    spec_ref, gains_ref, waves_ref, flips_ref, home_ref,
+    cells_in, green_in, pick_in, depth_table, waves_ref, flips_ref, home_ref,
+    cells_ref, field_ref, pick_ref, depth_ref, gains_ref, spec_ref,
     planes, green, freq, tables, flips,
-    fwd_send, fwd_recv, back_send, back_recv, green_send, green_recv, right_send, left_send, line_recv, own_sem, table_sem,
+    fwd_send, fwd_recv, back_send, back_recv, green_send, green_recv, right_send, left_send, line_recv, own_sem, table_sem, in_sem,
 ):
     groups = gy_count * gz_count
     rep, gy, gz = lax.axis_index("rep"), lax.axis_index("gy"), lax.axis_index("gz")
@@ -217,6 +229,14 @@
 
     def along(step):
         return {"rep": lax.rem(rep + step + reps, reps), "gy": gy, "gz": gz}
+
+    inputs = [
+        pltpu.make_async_copy(source, held, in_sem.at[i])
+        for i, (source, held) in enumerate((
+            (green_in, field_ref), (pick_in, pick_ref), (cells_in, cells_ref), (depth_table, depth_ref)))
+    ]
+    for copy in inputs:
+        copy.start()
 
     loads = []
     for table, (kind, swap) in enumerate(((1, False), (0, True), (0, False), (2, True))):
@@ -237,6 +257,9 @@
         pl.semaphore_signal(barrier, inc=1, device_id=partner(step)[1], device_id_type=MESH)
     for step in (1, -1):
         pl.semaphore_signal(barrier, inc=1, device_id=along(step), device_id_type=MESH)
+    for copy in inputs[:2]:
+        copy.wait()
+    pick_green(pick_ref, field_ref, gains_ref)
     pl.semaphore_wait(barrier, groups + 1)
 
     def green_copy(step, source, part):
@@ -271,7 +294,12 @@
     for part in range(PARTS):
         for step in order:
             green_copy(step, slot, part).start()
-    for copy in own_green + own_planes:
+    for copy in own_green:
+        copy.start()
+    for copy in inputs[2:]:
+        copy.wait()
+    depth_in(depth_ref, cells_ref, spec_ref)
+    for copy in own_planes:
         copy.start()
 
     def line_start(part):
@@ -430,18 +458,12 @@
     each = half // groups
     step = 8
     forward_table, back_table = depth_tables(depth, groups, each)
-    fwd_h, fwd_l = split_table(forward_table)
     back_h, back_l = split_table(back_table / (ng * ng * depth))
-    vmem = pl.BlockSpec(memory_space=pltpu.VMEM)
     table_spec = pl.BlockSpec((depth, depth), lambda i: (0, 0))
     cells_spec = pl.BlockSpec((step, cols, depth), lambda i: (i, 0, 0))
     spec_spec = pl.BlockSpec((groups, PARTS, step * 8, cols), lambda i: (0, 0, i, 0))
     spec_shape = jax.ShapeDtypeStruct((groups, PARTS, rows * 8, cols), f32)
-    limit = pltpu.CompilerParams(vmem_limit_bytes=40 * 2**20)
-    spec = pl.pallas_call(
-        depth_in_kernel, grid=(rows // step,), out_shape=spec_shape, name="depth_in",
-        in_specs=[table_spec, table_spec, cells_spec], out_specs=spec_spec, compiler_params=limit,
-    )(fwd_h, fwd_l, charges)
+    limit = pltpu.CompilerParams(vmem_limit_bytes=63 * 2**20)
 
     k1, k2, _ = green.shape
     own_index = np.arange(half)
@@ -450,19 +472,13 @@
     pick = np.zeros((2 * depth, depth), np.float32)
     pick[np.arange(depth), own_index[quads]] = 1.0
     pick[depth + np.arange(depth), opposite[quads]] = 1.0
-    gains = pl.pallas_call(
-        pick_kernel, out_shape=jax.ShapeDtypeStruct((groups, PARTS, k2 * 4, 2 * k1), f32), name="pick",
-        in_specs=[vmem, vmem], out_specs=vmem, compiler_params=limit,
-    )(jnp.asarray(pick, bf16), green.reshape(k1 * k2, depth))
-
     index = np.arange(ng)
     halves = np.concatenate([index[0::2], index[1::2]])
     angle = 2.0 * np.pi * ((index[:, None] * index[None, :]) % ng) / ng
     cos, sin = np.cos(angle), np.sin(angle)
     waves = np.stack([cos, sin, -sin])
     waves = np.concatenate([waves, waves[:, :, halves], waves[:, halves, :]])
-    rounded = waves.astype(jnp.bfloat16)
-    waves = jnp.asarray(np.stack([rounded, (waves - rounded.astype(np.float64)).astype(jnp.bfloat16)], axis=1))
+    waves = stacked_table(waves, 1)
     flips = np.stack([(rows_of[:, None] + rows_of[None, :]) % ng == 0 for rows_of in (index, halves)])
     flips = jnp.asarray(flips, bf16)
 
@@ -471,19 +487,25 @@
     home = pl.pallas_call(
         functools.partial(planes_kernel, gy_count, gz_count, reps),
         out_shape=spec_shape, name="planes",
-        in_specs=[pl.BlockSpec(memory_space=pl.ANY)] * 4, out_specs=pl.BlockSpec(memory_space=pl.ANY),
+        in_specs=[pl.BlockSpec(memory_space=pl.ANY)] * 6, out_specs=pl.BlockSpec(memory_space=pl.ANY),
         scratch_shapes=[
+            pltpu.VMEM(charges.shape, f32),
+            pltpu.VMEM((k1 * k2, depth), f32),
+            pltpu.VMEM(pick.shape, bf16),
+            pltpu.VMEM((2, depth, depth), bf16),
+            pltpu.VMEM((groups, PARTS, k2 * 4, 2 * k1), f32),
+            pltpu.VMEM(spec_shape.shape, f32),
             pltpu.VMEM(spec_shape.shape, f32),
             pltpu.VMEM((reps, PARTS, ng * each // PARTS, 2 * k1), f32),
             pltpu.VMEM((each, 2 * ng, ng), f32),
             pltpu.VMEM((4, 2, 2 * ng, 2 * ng), bf16),
             pltpu.VMEM((2, ng, ng), bf16),
             dma(both), dma(both), dma(both), dma(both), dma(both), dma(both),
-            dma((reps, PARTS)), dma((reps, PARTS)), dma((reps, PARTS)), dma((2 * PARTS,)), dma((17,)),
+            dma((reps, PARTS)), dma((reps, PARTS)), dma((reps, PARTS)), dma((2 * PARTS,)), dma((17,)), dma((4,)),
         ],
         compiler_params=pltpu.CompilerParams(
             collective_id=0, has_side_effects=True, vmem_limit_bytes=63 * 2**20),
-    )(spec, gains, waves, flips)
+    )(charges, green.reshape(k1 * k2, depth), jnp.asarray(pick, bf16), stacked_table(forward_table, 0), waves, flips)
 
     return pl.pallas_call(
         depth_out_kernel, grid=(rows // step,), out_shape=jax.ShapeDtypeStruct(charges.shape, f32), name="depth_out",

time: 133 us -> 120 us (0.902)
  local copies, waits for them, and re-layouts: 10.9 us -> 0 us
  Pallas kernels: 122 us -> 120 us
    unnamed x20 -> x0, local copies, waits for them, and re-layouts: 10.9 us -> none
    pallas_call x2 -> x0, Pallas kernels: 5.02 us -> none  [the longest x1 3.24 us: fused_plan(): pl.pallas_call(depth_in_kernel, grid=(rows // step,), out_shape=spec_shap...]
    pallas_call x1, Pallas kernels: 5.4 us -> 7.92 us  [fused_plan(): pl.pallas_call(depth_out_kernel, grid=(rows // step,), out_shape=jax.Shap...]
where the time goes in v2:
time: 120 us
  Pallas kernels  120 us (100%)
    pallas_call x1, Pallas kernels, fused_plan(): pl.pallas_call(functools.partial(planes_kernel, gy_count, gz_count, reps)...  112 us
    pallas_call x1, Pallas kernels, fused_plan(): pl.pallas_call(depth_out_kernel, grid=(rows // step,), out_shape=jax.Shap...  7.92 us

profile of v2, /device:TPU:0, one launch (start us, length us, event | category | flops | bytes accessed | tf_op | source)
XLA Modules:
  0.0 120.0 jit_solution(15840115219583125158)
XLA Ops:
  0.0 112.1 %planes.1.spec_ref = f32[8,2,512,128]{3,2,1,0:T(8,128)} custom-call(f32[64,128,128]{2,1,0:T(8,128)} %cells_in.1, f32[2048,128]{1,0:T(8,128)} %bitcast.1, bf16[256,128]{1,0:T(8,128)(2,1)} %constant.16.clone.pick_in, bf16[2,128,128]{2,1,0:T(8,128)(2,1)} %constant.17.clone.depth_table, bf16[9,2,256,256]{3,2,1,0:T(8,128)(2,1)} %constant.14.clone.waves_ref, ...), custom_call_target="tpu_custom_call" | custom-call | tf_op jit(solution)/shard_map/planes/pallas_call | solution.py:487
  112.1 7.9 %depth_out.1 = f32[64,128,128]{2,1,0:T(8,128)} custom-call(bf16[128,128]{1,0:T(8,128)(2,1)} %constant.12.clone.high_ref, bf16[128,128]{1,0:T(8,128)(2,1)} %constant.13.clone.low_ref, f32[8,2,512,128]{3,2,1,0:T(8,128)} %planes.1.spec_ref), custom_call_target="tpu_custom_call" | custom-call | tf_op jit(solution)/shard_map/depth_out/pallas_call | solution.py:510
